TPU v7x, 32 devices: a whole 2x2x4 slice. The times are simulated.
32 devices in a mesh: grp: 4 (over y, core), brk: 8 (over z, x).
Axes of the slice: x: 2, y: 2, z: 4, core: 2. Of those that a mesh axis runs over, the one named last changes fastest.
Arguments:
- field: float32 [5, 64, 128, 128], P(None, 'brk', 'grp'), may hold values from -6 to 6
- donors: float32 [1024, 640], P(('grp', 'brk')), may hold values from -6 to 6
- donor_block: int32 [4, 8, 8, 128], P('grp', 'brk'), may hold values from 0 to 31
- donor_corner: int32 [4, 8, 8, 128], P('grp', 'brk'), may hold values from 0 to 86, as said below
- donor_weight: float32 [3, 4, 8, 8, 128], P(None, 'grp', 'brk'), may hold values from 0 to 1
- fringe_count: int32 [4, 8, 8], P('grp', 'brk'), may hold values from 64 to 128, as said below
- fringe_cell: int32 [4, 8, 8, 128], P('grp', 'brk'), may hold values from 0 to 32767, as said below
- velocity: float32 [3, 5], replicated, may hold values from -1 to 1
- mixing: float32 [5, 5], replicated, may hold values from -1.5 to 1.5
Outputs:
- advanced: float32 [5, 64, 128, 128], P(None, 'brk', 'grp')
Inputs may be any that keep to these rules, and one draw needn't show every extreme that they name: `fringe_cell`: within one brick the receiving cells of all slots are distinct. `fringe_count`: each brick has an owner with exactly 128 live slots, and in each group some owner has 128 live slots from every brick of the group. `donor_corner`: the corner is 32 ox + 8 oy + oz with ox and oy in 0 to 2 and oz in 0 to 6.
All inputs are finite; a program needn't handle non-finite values.
Results may differ from a plain program's by a relative error of at most 0.0003.
Values sent between devices are 32-bit elements; how exact they have to be, the bound alone decides.
A program may use at most 64 MiB of HBM per device.

v0:
```python
import functools

import jax
import jax.numpy as jnp
from jax import lax
from jax.experimental import pallas as pl
from jax.experimental.pallas import tpu as pltpu
from jax.sharding import PartitionSpec as P

time_step = 0.3
PLUS = (-2.0 / 60, 15.0 / 60, -60.0 / 60, 20.0 / 60, 30.0 / 60, -3.0 / 60, 0.0)
MINUS = (0.0, 3.0 / 60, -30.0 / 60, -20.0 / 60, 60.0 / 60, -15.0 / 60, 2.0 / 60)
NT = (((1,), (1,)), ((), ()))


def send(src, dst, sems, index, where):
    copy = pltpu.make_async_remote_copy(
        src_ref=src,
        dst_ref=dst,
        send_sem=sems[0].at[index],
        recv_sem=sems[1].at[index],
        device_id=where,
        device_id_type=pl.DeviceIdType.MESH,
    )
    copy.start()
    return copy


def factors(low, weight, count):
    return [
        jnp.where(low == c, 1.0 - weight, jnp.where(low == c - 1, weight, 0.0))
        for c in range(count)
    ]


def kernel(
    n_grp, n_brk, field, donors, blk, corner, weight, counts, cells, velocity, mixing, out,
    req, req_in, res, val_in, cell_out, cell_in, turned, rows_hot, lanes_hot, rows_side,
    lanes_side, u0, y0, u1, y1, faces, ysend, yrecv, coef, send_sems, recv_sems,
):
    nvars, cx, cy, cz = field.shape
    nblk = donors.shape[0]
    block = donors.shape[1] // nvars
    sems = (send_sems, recv_sems)
    g = lax.axis_index("grp")
    b = lax.axis_index("brk")
    up_b, down_b = lax.rem(b + 1, n_brk), lax.rem(b + n_brk - 1, n_brk)
    up_g, down_g = lax.rem(g + 1, n_grp), lax.rem(g + n_grp - 1, n_grp)

    barrier = pltpu.get_barrier_semaphore()
    for k in range(1, n_brk):
        pl.semaphore_signal(
            barrier, inc=1, device_id=(g, lax.rem(b + k, n_brk)),
            device_id_type=pl.DeviceIdType.MESH,
        )
    for other in (up_g, down_g):
        pl.semaphore_signal(
            barrier, inc=1, device_id=(other, b), device_id_type=pl.DeviceIdType.MESH
        )

    blank = jnp.zeros((3, cz), jnp.float32)
    for o in range(n_brk):
        req[o] = jnp.concatenate(
            [
                blk[o : o + 1].astype(jnp.float32),
                corner[o : o + 1].astype(jnp.float32),
                weight[0, o : o + 1],
                weight[1, o : o + 1],
                weight[2, o : o + 1],
                blank,
            ],
            axis=0,
        )
    req_in[b] = req[b]
    slots = cz
    slot_id = lax.broadcasted_iota(jnp.int32, (1, slots), 1)
    for o in range(n_brk):
        cell_out[o : o + 1] = jnp.where(slot_id < counts[o], cells[o : o + 1], -1)
    for v in range(nvars):
        center = 0.0
        for d in range(3):
            speed = velocity[d, v]
            fast = jnp.maximum(speed, 0.0) * (-time_step)
            slow = jnp.minimum(speed, 0.0) * (-time_step)
            for k in range(7):
                value = fast * PLUS[k] + slow * MINUS[k]
                if k == 3:
                    center = center + value
                else:
                    coef[v, d * 7 + k] = value
        coef[v, 3] = center
        for w in range(nvars):
            coef[v, 21 + w] = mixing[v, w] * (-time_step)

    pl.semaphore_wait(barrier, n_brk + 1)
    copies = []
    asks = []
    for k in range(1, n_brk):
        o = lax.rem(b + k, n_brk)
        asks.append(send(req.at[o], req_in.at[b], sems, k, (g, o)))
    base = n_brk
    targets = [
        send(cell_out, cell_in.at[0], sems, base, (g, up_b)),
        send(cell_out, cell_in.at[1], sems, base + 1, (g, down_b)),
    ]
    base = base + 2
    raw = []

    def send_raw(v):
        raw.append(
            send(
                field.at[v, pl.ds(cx - 3, 3)], u0.at[v, pl.ds(0, 3)], sems, base + 2 * v,
                (g, up_b),
            )
        )
        raw.append(
            send(
                field.at[v, pl.ds(0, 3)], u0.at[v, pl.ds(cx + 3, 3)], sems, base + 2 * v + 1,
                (g, down_b),
            )
        )

    for v in range(2):
        send_raw(v)
    value_base = base + 2 * nvars
    exchange_base = value_base + 3 * n_brk

    whole = donors[...]
    first = whole.astype(jnp.bfloat16).astype(jnp.float32)
    second = (whole - first).astype(jnp.bfloat16).astype(jnp.float32)
    third = whole - first - second
    stacked = jnp.concatenate([first, second, third, jnp.zeros_like(whole)], axis=0)
    turned[...] = jnp.transpose(stacked).astype(jnp.bfloat16)

    def mark(targets_ref, top, height, rows_ref, lanes_ref):
        row_id = lax.broadcasted_iota(jnp.int32, (height, slots), 0)
        lane_id = lax.broadcasted_iota(jnp.int32, (cz, slots), 0)
        for o in range(n_brk):
            cell = targets_ref[o : o + 1]
            row = jnp.where(cell < 0, -1, cell // cz - top)
            part = slice(o * slots, (o + 1) * slots)
            rows_ref[:, part] = jnp.where(row_id == row, 1.0, 0.0).astype(jnp.bfloat16)
            lanes_ref[:, part] = jnp.where(lane_id == cell % cz, 1.0, 0.0).astype(jnp.bfloat16)
        return lax.dot_general(
            rows_ref[...], lanes_ref[...], NT, preferred_element_type=jnp.float32
        )

    covered = mark(cell_out, 0, cx * cy, rows_hot, lanes_hot)

    block_id = lax.broadcasted_iota(jnp.int32, (4 * nblk, slots), 0) % nblk

    def interpolated(r):
        asked = req_in[r]
        wanted = asked[0:1].astype(jnp.int32)
        low = asked[1:2].astype(jnp.int32)
        hot = jnp.where(block_id == wanted, 1.0, 0.0).astype(jnp.bfloat16)
        picked = jnp.dot(turned[...], hot, preferred_element_type=jnp.float32)
        fx = factors(low // 32, asked[2:3], 4)
        fy = factors((low // 8) % 4, asked[3:4], 4)
        z_id = lax.broadcasted_iota(jnp.int32, (8, slots), 0)
        low_z = low % 8
        wz = asked[4:5]
        fz = jnp.where(z_id == low_z, 1.0 - wz, jnp.where(z_id == low_z + 1, wz, 0.0))
        tables = [fx[i] * fy[j] * fz for i in range(4) for j in range(4)]
        sums = []
        for v in range(nvars):
            total = None
            for i, table in enumerate(tables):
                start = v * block + 8 * i
                term = picked[start : start + 8] * table
                total = term if total is None else total + term
            sums.append(jnp.sum(total, axis=0, keepdims=True))
        return jnp.concatenate(sums + [blank], axis=0)

    answers = []

    for k in range(n_brk):
        if k > 0:
            asks[k - 1].wait_recv()
        r = lax.rem(b + n_brk - k, n_brk)
        res[r + 1] = interpolated(r)
    res[0] = res[n_brk]
    res[n_brk + 1] = res[1]
    for k in range(1, n_brk):
        o = lax.rem(b + k, n_brk)
        answers.append(
            send(res.at[pl.ds(o, 3)], val_in.at[b], sems, value_base + k, (g, o))
        )
    for v in range(2, nvars):
        send_raw(v)
    for slot in range(3):
        val_in[b, slot] = res[b + slot]
    covered_side = []
    for side, top in ((0, (cx - 3) * cy), (1, 0)):
        targets[side].wait_recv()
        covered_side.append(
            mark(cell_in.at[side], top, 3 * cy, rows_side.at[side], lanes_side.at[side])
        )
    for pending in answers:
        pending.wait_recv()

    def placed(slot, v, rows, lanes):
        row = jnp.concatenate([val_in[o, slot, v : v + 1] for o in range(n_brk)], axis=1)
        high = row.astype(jnp.bfloat16)
        rest = (row - high.astype(jnp.float32)).astype(jnp.bfloat16)
        spread = jnp.concatenate([lanes * high, lanes * rest], axis=0)
        both = lax.dot_general(rows, spread, NT, preferred_element_type=jnp.float32)
        return both[:, :cz] + both[:, cz:]

    for v in range(nvars):
        landed = placed(1, v, rows_hot[...], lanes_hot[...])
        for x in range(cx):
            part = slice(x * cy, (x + 1) * cy)
            plane = jnp.where(covered[part] > 0.5, landed[part], field[v, x])
            u0[v, 3 + x] = plane
            y0[v, x, 8 : 8 + cy] = plane

    def send_y(stage, y):
        for v in range(nvars):
            for k in range(3):
                ysend[stage, 0, k, v] = y[v, :, 8 + cy - 3 + k, :]
                ysend[stage, 1, k, v] = y[v, :, 8 + k, :]
        first = exchange_base + 4 * stage
        return [
            send(ysend.at[stage, 0], yrecv.at[stage, 0], sems, first, (up_g, b)),
            send(ysend.at[stage, 1], yrecv.at[stage, 1], sems, first + 1, (down_g, b)),
        ]

    def land_y(stage, y, pending):
        for copy in pending:
            copy.wait_recv()
        for v in range(nvars):
            for k in range(3):
                y[v, :, 5 + k, :] = yrecv[stage, 0, k, v]
                y[v, :, 8 + cy + k, :] = yrecv[stage, 1, k, v]
        copies.extend(pending)

    def section(u, y, store, start, stop):
        def plane(x, carry):
            centers = [u[v, x + 3] for v in range(nvars)]
            for v in range(nvars):
                total = coef[v, 3] * centers[v]
                for k in (0, 1, 2, 4, 5, 6):
                    total = total + coef[v, k] * u[v, x + k]
                    total = total + coef[v, 7 + k] * y[v, x, 5 + k : 5 + k + cy]
                    total = total + coef[v, 14 + k] * pltpu.roll(
                        centers[v], (3 - k) % cz, 1
                    )
                for w in range(nvars):
                    total = total + coef[v, 21 + w] * centers[w]
                store(x, v, centers[v] + total)
            return carry

        lax.fori_loop(start, stop, plane, 0)

    def store_first(x, v, value):
        u1[v, x + 3] = value
        y1[v, x, 8 : 8 + cy] = value

    def store_last(x, v, value):
        out[v, x] = 0.5 * u0[v, x + 3] + 0.5 * value

    y_pending = send_y(0, y0)
    for copy in raw:
        copy.wait_recv()
    for side, slot, start in ((0, 0, 0), (1, 2, cx + 3)):
        for v in range(nvars):
            landed = placed(slot, v, rows_side[side], lanes_side[side])
            for x in range(3):
                part = slice(x * cy, (x + 1) * cy)
                u0[v, start + x] = jnp.where(
                    covered_side[side][part] > 0.5, landed[part], u0[v, start + x]
                )
    land_y(0, y0, y_pending)

    section(u0, y0, store_first, 0, 3)
    section(u0, y0, store_first, cx - 3, cx)
    first = exchange_base + 2
    x_pending = [
        send(u1.at[:, pl.ds(cx, 3)], faces.at[0], sems, first, (g, up_b)),
        send(u1.at[:, pl.ds(3, 3)], faces.at[1], sems, first + 1, (g, down_b)),
    ]
    section(u0, y0, store_first, 3, cx - 3)
    y_pending = send_y(1, y1)
    zero = jnp.zeros((cy, cz), jnp.float32)
    for v in range(nvars):
        for x in range(3):
            u1[v, x] = zero
            u1[v, cx + 3 + x] = zero
    land_y(1, y1, y_pending)
    section(u1, y1, store_last, 0, cx)
    for copy in x_pending:
        copy.wait_recv()
    for v in range(nvars):
        for x in range(3):
            low = out[v, x]
            for k in range(3 - x):
                low = low + (0.5 * coef[v, k]) * faces[0, v, x + k]
            out[v, x] = low
            top = out[v, cx - 1 - x]
            for k in range(3 - x):
                top = top + (0.5 * coef[v, 6 - k]) * faces[1, v, 2 - x - k]
            out[v, cx - 1 - x] = top
    for copy in copies + asks + targets + raw + answers + x_pending:
        copy.wait_send()


def body(
    n_grp, n_brk, field, donors, donor_block, donor_corner, donor_weight, fringe_count,
    fringe_cell, velocity, mixing,
):
    nvars, cx, cy, cz = field.shape
    owners, slots = donor_block.shape[2:]
    vmem = pl.BlockSpec(memory_space=pltpu.VMEM)
    smem = pl.BlockSpec(memory_space=pltpu.SMEM)
    f32 = jnp.float32
    nsem = 4 * n_brk + 2 + 2 * nvars + 8
    return pl.pallas_call(
        functools.partial(kernel, n_grp, n_brk),
        out_shape=jax.ShapeDtypeStruct(field.shape, f32),
        in_specs=[vmem] * 5 + [smem, vmem, smem, smem],
        out_specs=vmem,
        scratch_shapes=[
            pltpu.VMEM((owners, 8, slots), f32),
            pltpu.VMEM((owners, 8, slots), f32),
            pltpu.VMEM((owners + 2, 8, slots), f32),
            pltpu.VMEM((owners, 3, 8, slots), f32),
            pltpu.VMEM((owners, slots), jnp.int32),
            pltpu.VMEM((2, owners, slots), jnp.int32),
            pltpu.VMEM((donors.shape[1], 4 * donors.shape[0]), jnp.bfloat16),
            pltpu.VMEM((cx * cy, owners * slots), jnp.bfloat16),
            pltpu.VMEM((cz, owners * slots), jnp.bfloat16),
            pltpu.VMEM((2, 3 * cy, owners * slots), jnp.bfloat16),
            pltpu.VMEM((2, cz, owners * slots), jnp.bfloat16),
            pltpu.VMEM((nvars, cx + 6, cy, cz), f32),
            pltpu.VMEM((nvars, cx, cy + 16, cz), f32),
            pltpu.VMEM((nvars, cx + 6, cy, cz), f32),
            pltpu.VMEM((nvars, cx, cy + 16, cz), f32),
            pltpu.VMEM((2, nvars, 3, cy, cz), f32),
            pltpu.VMEM((2, 2, 3, nvars, cx, cz), f32),
            pltpu.VMEM((2, 2, 3, nvars, cx, cz), f32),
            pltpu.SMEM((nvars, 21 + nvars), f32),
            pltpu.SemaphoreType.DMA((nsem,)),
            pltpu.SemaphoreType.DMA((nsem,)),
        ],
        compiler_params=pltpu.CompilerParams(collective_id=0, has_side_effects=True),
    )(
        field, donors, donor_block.reshape(owners, slots), donor_corner.reshape(owners, slots),
        donor_weight.reshape(3, owners, slots), fringe_count.reshape(owners),
        fringe_cell.reshape(owners, slots), velocity, mixing,
    )


def solution(mesh):
    placed = (
        P(None, "brk", "grp", None),
        P(("grp", "brk"), None),
        P("grp", "brk", None, None),
        P("grp", "brk", None, None),
        P(None, "grp", "brk", None, None),
        P("grp", "brk", None),
        P("grp", "brk", None, None),
        P(),
        P(),
    )
    return jax.shard_map(
        functools.partial(body, mesh.shape["grp"], mesh.shape["brk"]),
        mesh=mesh, in_specs=placed, out_specs=P(None, "brk", "grp", None), check_vma=False,
    )
```

profile of v0, /device:TPU:0, one launch (start us, length us, event | category | flops | bytes accessed | tf_op | source)
XLA Modules:
  0.0 40.2 jit_solution(148029490156342642)
XLA Ops:
  0.0 38.2 %shard_map.91 = f32[5,8,32,128]{3,2,1,0:T(8,128)} custom-call(f32[5,8,32,128]{3,2,1,0:T(8,128)} %field.1, f32[32,640]{1,0:T(8,128)} %donors.1, s32[8,128]{1,0:T(8,128)} %bitcast.6, s32[8,128]{1,0:T(8,128)} %bitcast.7, f32[3,8,128]{2,1,0:T(8,128)} %bitcast.5, s32[8]{0:T(128)} %bitcast.9, s32[8,128]{1,0:T(8,128)} %bitcast.8, f32[3,5]{1,0:T(4,128)} %velocity.1, ...), custom_call_target="tpu_custom_call" | custom-call | tf_op jit(solution)/shard_map/pallas_call | solution.py:318
  38.2 2.0 %copy.11 = f32[5,8,32,128]{3,2,1,0:T(8,128)} copy(f32[5,8,32,128]{3,2,1,0:T(8,128)} %shard_map.91) | data formatting | bytes 1310720
where the time goes:
time: 40.3 us; the launch traced here: 40.2 us
  Pallas kernels  38.2 us (95%)
  local copies, waits for them, and re-layouts  1.99 us (5%)
    pallas_call x1, Pallas kernels, body(): pl.pallas_call(functools.partial(kernel, n_grp, n_brk), out_shape=jax.Sha...  38.2 us
    unnamed x1, local copies, waits for them, and re-layouts  1.99 us

commit v1 on v0

--- a/solution.py
+++ b/solution.py
@@ -34,10 +34,23 @@
 
 
 def kernel(
-    n_grp, n_brk, field, donors, blk, corner, weight, counts, cells, velocity, mixing, out,
-    req, req_in, res, val_in, cell_out, cell_in, turned, rows_hot, lanes_hot, rows_side,
+    n_grp, n_brk, field_in, donors_in, blk_in, corner_in, weight_in, counts_in, cells_in,
+    velocity_in, mixing_in, out, field, donors, blk, corner, weight, counts, cells, velocity,
+    mixing, in_sems, req, req_in, res, val_in, cell_out, cell_in, turned, rows_hot, lanes_hot, rows_side,
     lanes_side, u0, y0, u1, y1, faces, ysend, yrecv, coef, send_sems, recv_sems,
 ):
+    loads = [
+        pltpu.make_async_copy(src, dst, in_sems.at[i])
+        for i, (src, dst) in enumerate(
+            (
+                (blk_in, blk), (corner_in, corner), (weight_in, weight), (counts_in, counts),
+                (cells_in, cells), (velocity_in, velocity), (mixing_in, mixing),
+                (donors_in, donors), (field_in, field),
+            )
+        )
+    ]
+    for load in loads:
+        load.start()
     nvars, cx, cy, cz = field.shape
     nblk = donors.shape[0]
     block = donors.shape[1] // nvars
@@ -58,6 +71,8 @@
             barrier, inc=1, device_id=(other, b), device_id_type=pl.DeviceIdType.MESH
         )
 
+    for load in loads[:-1]:
+        load.wait()
     blank = jnp.zeros((3, cz), jnp.float32)
     for o in range(n_brk):
         req[o] = jnp.concatenate(
@@ -92,6 +107,7 @@
         for w in range(nvars):
             coef[v, 21 + w] = mixing[v, w] * (-time_step)
 
+    loads[-1].wait()
     pl.semaphore_wait(barrier, n_brk + 1)
     copies = []
     asks = []
@@ -312,15 +328,26 @@
     nvars, cx, cy, cz = field.shape
     owners, slots = donor_block.shape[2:]
     vmem = pl.BlockSpec(memory_space=pltpu.VMEM)
-    smem = pl.BlockSpec(memory_space=pltpu.SMEM)
+    hbm = pl.BlockSpec(memory_space=pltpu.HBM)
+    i32 = jnp.int32
     f32 = jnp.float32
     nsem = 4 * n_brk + 2 + 2 * nvars + 8
     return pl.pallas_call(
         functools.partial(kernel, n_grp, n_brk),
         out_shape=jax.ShapeDtypeStruct(field.shape, f32),
-        in_specs=[vmem] * 5 + [smem, vmem, smem, smem],
+        in_specs=[hbm] * 9,
         out_specs=vmem,
         scratch_shapes=[
+            pltpu.VMEM(field.shape, f32),
+            pltpu.VMEM(donors.shape, f32),
+            pltpu.VMEM((owners, slots), i32),
+            pltpu.VMEM((owners, slots), i32),
+            pltpu.VMEM((3, owners, slots), f32),
+            pltpu.SMEM((owners,), i32),
+            pltpu.VMEM((owners, slots), i32),
+            pltpu.SMEM(velocity.shape, f32),
+            pltpu.SMEM(mixing.shape, f32),
+            pltpu.SemaphoreType.DMA((9,)),
             pltpu.VMEM((owners, 8, slots), f32),
             pltpu.VMEM((owners, 8, slots), f32),
             pltpu.VMEM((owners + 2, 8, slots), f32),
@@ -343,11 +370,19 @@
             pltpu.SemaphoreType.DMA((nsem,)),
             pltpu.SemaphoreType.DMA((nsem,)),
         ],
-        compiler_params=pltpu.CompilerParams(collective_id=0, has_side_effects=True),
+        compiler_params=pltpu.CompilerParams(
+            collective_id=0, has_side_effects=True, vmem_limit_bytes=32 << 20
+        ),
     )(
-        field, donors, donor_block.reshape(owners, slots), donor_corner.reshape(owners, slots),
-        donor_weight.reshape(3, owners, slots), fringe_count.reshape(owners),
-        fringe_cell.reshape(owners, slots), velocity, mixing,
+        *[
+            pltpu.with_memory_space_constraint(x, pltpu.HBM)
+            for x in (
+                field, donors, donor_block.reshape(owners, slots),
+                donor_corner.reshape(owners, slots), donor_weight.reshape(3, owners, slots),
+                fringe_count.reshape(owners), fringe_cell.reshape(owners, slots), velocity,
+                mixing,
+            )
+        ]
     )
 
 

time: 40.3 us -> 37.2 us (0.923)
  Pallas kernels: 38.2 us -> 36.2 us
  local copies, waits for them, and re-layouts: 1.99 us -> 0.84 us
    pallas_call x1, Pallas kernels: 38.2 us -> 36.2 us  [body(): pl.pallas_call(functools.partial(kernel, n_grp, n_brk), out_shape=jax.Sha...]
    unnamed x1, local copies, waits for them, and re-layouts: 1.99 us -> 0.84 us
where the time goes in v1:
time: 37.2 us; the launch traced here: 37.1 us
  Pallas kernels  36.2 us (97%)
  local copies, waits for them, and re-layouts  0.84 us (2%)
    pallas_call x1, Pallas kernels, body(): pl.pallas_call(functools.partial(kernel, n_grp, n_brk), out_shape=jax.Sha...  36.2 us
    unnamed x1, local copies, waits for them, and re-layouts  0.84 us

profile of v1, /device:TPU:0, one launch (start us, length us, event | category | flops | bytes accessed | tf_op | source)
XLA Modules:
  0.0 37.1 jit_solution(10718002415199965106)
XLA Ops:
  0.0 36.2 %shard_map.91 = f32[5,8,32,128]{3,2,1,0:T(8,128)S(1)} custom-call(f32[5,8,32,128]{3,2,1,0:T(8,128)} %field_in.1, f32[32,640]{1,0:T(8,128)} %donors_in.1, s32[8,128]{1,0:T(8,128)} %bitcast.6, s32[8,128]{1,0:T(8,128)} %bitcast.7, f32[3,8,128]{2,1,0:T(8,128)} %bitcast.5, s32[8]{0:T(128)} %bitcast.9, s32[8,128]{1,0:T(8,128)} %bitcast.8, f32[3,5]{1,0:T(4,128)} %velocity_in.1, ...), custom_call_target="tpu_custom_call" | custom-call | tf_op jit(solution)/shard_map/pallas_call | solution.py:335
  36.2 0.8 %copy.11 = f32[5,8,32,128]{3,2,1,0:T(8,128)} copy(f32[5,8,32,128]{3,2,1,0:T(8,128)S(1)} %shard_map.91) | data formatting | bytes 1310720

commit v2 on v1

v2 whole, which is shorter than its diff:
```python
import functools

import jax
import jax.numpy as jnp
from jax import lax
from jax.experimental import pallas as pl
from jax.experimental.pallas import tpu as pltpu
from jax.sharding import PartitionSpec as P

time_step = 0.3
PLUS = (-2.0 / 60, 15.0 / 60, -60.0 / 60, 20.0 / 60, 30.0 / 60, -3.0 / 60, 0.0)
MINUS = (0.0, 3.0 / 60, -30.0 / 60, -20.0 / 60, 60.0 / 60, -15.0 / 60, 2.0 / 60)
NT = (((1,), (1,)), ((), ()))
REACH = 3
DEEP = 2 * REACH
EDGE = 8
PAD = 2 * EDGE


def factors(low, weight, count):
    return [
        jnp.where(low == c, 1.0 - weight, jnp.where(low == c - 1, weight, 0.0))
        for c in range(count)
    ]


def kernel(
    n_grp, n_brk, field_in, donors_in, blk_in, corner_in, weight_in, counts_in, cells_in,
    velocity_in, mixing_in, out, field, donors, blk, corner, weight, counts, cells, velocity,
    mixing, req, req_in, res, val_in, cell_out, cell_in, turned, rows_hot, lanes_hot, rows_side,
    lanes_side, u, first, relay, coef, in_sems, send_sems, recv_sems,
):
    nvars, cx, cy, cz = field_in.shape
    nblk = donors.shape[0]
    block = donors.shape[1] // nvars
    slots = cz
    g = lax.axis_index("grp")
    b = lax.axis_index("brk")
    odd = lax.rem(b, 2)
    partner = b + 1 - 2 * odd
    other = lax.rem(b + n_brk - 1 + 2 * odd, n_brk)
    onward = lax.rem(b + n_brk + 2 - 4 * odd, n_brk)
    up_g, down_g = lax.rem(g + 1, n_grp), lax.rem(g + n_grp - 1, n_grp)
    own = pl.ds(PAD, cy)

    def natural(p):
        return p + odd * (cx - 1 - 2 * p)

    loads = [
        pltpu.make_async_copy(src, dst, in_sems.at[i])
        for i, (src, dst) in enumerate(
            [
                (blk_in, blk), (corner_in, corner), (weight_in, weight), (counts_in, counts),
                (cells_in, cells), (velocity_in, velocity), (mixing_in, mixing),
                (donors_in, donors),
            ]
            + [(field_in.at[:, natural(p)], field.at[p]) for p in range(cx)]
        )
    ]
    for load in loads:
        load.start()

    barrier = pltpu.get_barrier_semaphore()
    for k in range(1, n_brk):
        pl.semaphore_signal(
            barrier, inc=1, device_id=(g, lax.rem(b + k, n_brk)),
            device_id_type=pl.DeviceIdType.MESH,
        )
    for where in (up_g, down_g):
        pl.semaphore_signal(
            barrier, inc=1, device_id=(where, b), device_id_type=pl.DeviceIdType.MESH
        )

    index = [0]
    started = []

    def send(src, dst, where):
        i = index[0]
        index[0] = i + 1
        copy = pltpu.make_async_remote_copy(
            src_ref=src, dst_ref=dst, send_sem=send_sems.at[i], recv_sem=recv_sems.at[i],
            device_id=where, device_id_type=pl.DeviceIdType.MESH,
        )
        copy.start()
        started.append(copy)
        return copy

    for load in loads[:8]:
        load.wait()
    blank = jnp.zeros((3, slots), jnp.float32)
    for o in range(n_brk):
        req[o] = jnp.concatenate(
            [
                blk[o : o + 1].astype(jnp.float32),
                corner[o : o + 1].astype(jnp.float32),
                weight[0, o : o + 1],
                weight[1, o : o + 1],
                weight[2, o : o + 1],
                blank,
            ],
            axis=0,
        )
    req_in[b] = req[b]
    slot_id = lax.broadcasted_iota(jnp.int32, (1, slots), 1)
    for o in range(n_brk):
        cell_out[o : o + 1] = jnp.where(slot_id < counts[o], cells[o : o + 1], -1)
    for v in range(nvars):
        center = 0.0
        for d in range(3):
            speed = velocity[d, v]
            fast = jnp.maximum(speed, 0.0) * (-time_step)
            slow = jnp.minimum(speed, 0.0) * (-time_step)
            for k in range(7):
                value = fast * PLUS[k] + slow * MINUS[k]
                if d == 0:
                    value = jnp.where(odd == 1, fast * PLUS[6 - k] + slow * MINUS[6 - k], value)
                if k == 3:
                    center = center + value
                else:
                    coef[v, d * 7 + k] = value
        coef[v, 3] = center
        for w in range(nvars):
            coef[v, 21 + w] = mixing[v, w] * (-time_step)
    for load in loads[8:]:
        load.wait()
    pl.semaphore_wait(barrier, n_brk + 1)

    asks = []
    for k in range(1, n_brk):
        o = lax.rem(b + k, n_brk)
        asks.append(send(req.at[o], req_in.at[b], (g, o)))
    cells_sent = [
        send(cell_out, cell_in.at[0], (g, other)), send(cell_out, cell_in.at[1], (g, partner))
    ]
    mirror = DEEP + 2 * cx - 1
    direct = {}

    def give(p, blended):
        src = u.at[DEEP + p, :, own] if blended else field.at[p]
        dst = u.at[mirror - p, :, own] if p >= cx - DEEP else relay.at[p]
        direct[p] = send(src, dst, (g, partner))

    passed = {}

    def pass_on(p):
        direct[p].wait_recv()
        src = u.at[mirror - p, :, own] if p >= cx - DEEP else relay.at[p]
        passed[p] = send(src, u.at[DEEP - 1 - p, :, own], (g, onward))

    give(0, False)
    give(1, False)

    whole = donors[...]
    one = whole.astype(jnp.bfloat16).astype(jnp.float32)
    two = (whole - one).astype(jnp.bfloat16).astype(jnp.float32)
    three = whole - one - two
    stacked = jnp.concatenate([one, two, three, jnp.zeros_like(whole)], axis=0)
    turned[...] = jnp.transpose(stacked).astype(jnp.bfloat16)

    def mark(targets_ref, flip, top, height, rows_ref, lanes_ref):
        row_id = lax.broadcasted_iota(jnp.int32, (height, slots), 0)
        lane_id = lax.broadcasted_iota(jnp.int32, (cz, slots), 0)
        for o in range(n_brk):
            cell = targets_ref[o : o + 1]
            row = cell // cz
            x = row // cy
            row = row + (flip * (cx - 1 - 2 * x) - top) * cy
            row = jnp.where(cell < 0, -1, row)
            part = slice(o * slots, (o + 1) * slots)
            rows_ref[:, part] = jnp.where(row_id == row, 1.0, 0.0).astype(jnp.bfloat16)
            lanes_ref[:, part] = jnp.where(lane_id == cell % cz, 1.0, 0.0).astype(jnp.bfloat16)
        return lax.dot_general(
            rows_ref[...], lanes_ref[...], NT, preferred_element_type=jnp.float32
        )

    covered = mark(cell_out, odd, 0, cx * cy, rows_hot, lanes_hot)

    block_id = lax.broadcasted_iota(jnp.int32, (4 * nblk, slots), 0) % nblk

    def interpolated(r):
        asked = req_in[r]
        wanted = asked[0:1].astype(jnp.int32)
        low = asked[1:2].astype(jnp.int32)
        hot = jnp.where(block_id == wanted, 1.0, 0.0).astype(jnp.bfloat16)
        picked = jnp.dot(turned[...], hot, preferred_element_type=jnp.float32)
        fx = factors(low // 32, asked[2:3], 4)
        fy = factors((low // 8) % 4, asked[3:4], 4)
        z_id = lax.broadcasted_iota(jnp.int32, (8, slots), 0)
        low_z = low % 8
        wz = asked[4:5]
        fz = jnp.where(z_id == low_z, 1.0 - wz, jnp.where(z_id == low_z + 1, wz, 0.0))
        tables = [fx[i] * fy[j] * fz for i in range(4) for j in range(4)]
        sums = []
        for v in range(nvars):
            total = None
            for i, table in enumerate(tables):
                start = v * block + 8 * i
                term = picked[start : start + 8] * table
                total = term if total is None else total + term
            sums.append(jnp.sum(total, axis=0, keepdims=True))
        return jnp.concatenate(sums + [blank], axis=0)

    for k in range(n_brk):
        if k > 0:
            asks[k - 1].wait_recv()
        r = lax.rem(b + n_brk - k, n_brk)
        res[r + 1] = interpolated(r)
    res[0] = res[n_brk]
    res[n_brk + 1] = res[1]
    answers = []
    for k in range(1, n_brk):
        o = lax.rem(b + k, n_brk)
        answers.append(send(res.at[pl.ds(o, 3)], val_in.at[b], (g, o)))
    give(cx - 1, False)
    give(cx - 2, False)
    for slot in range(3):
        val_in[b, slot] = res[b + slot]

    covered_side = []
    for side, top in ((0, 0), (1, cx - 2)):
        cells_sent[side].wait_recv()
        covered_side.append(
            mark(cell_in.at[side], 1 - odd, top, 2 * cy, rows_side.at[side], lanes_side.at[side])
        )
    pass_on(0)
    pass_on(1)
    for pending in answers:
        pending.wait_recv()

    def placed(slot, v, rows, lanes):
        row = jnp.concatenate([val_in[o, slot, v : v + 1] for o in range(n_brk)], axis=1)
        high = row.astype(jnp.bfloat16)
        rest = (row - high.astype(jnp.float32)).astype(jnp.bfloat16)
        spread = jnp.concatenate([lanes * high, lanes * rest], axis=0)
        both = lax.dot_general(rows, spread, NT, preferred_element_type=jnp.float32)
        return both[:, :cz] + both[:, cz:]

    for v in range(nvars):
        landed = placed(1, v, rows_hot[...], lanes_hot[...])
        for p in range(cx):
            part = slice(p * cy, (p + 1) * cy)
            u[DEEP + p, v, PAD : PAD + cy] = jnp.where(
                covered[part] > 0.5, landed[part], field[p, v]
            )
    for p in (2, 5, 3, 4):
        give(p, True)

    def edges(positions):
        return [
            send(
                u.at[positions, :, pl.ds(PAD + cy - EDGE, EDGE)],
                u.at[positions, :, pl.ds(PAD - EDGE, EDGE)], (up_g, b),
            ),
            send(
                u.at[positions, :, pl.ds(PAD, EDGE)],
                u.at[positions, :, pl.ds(PAD + cy, EDGE)], (down_g, b),
            ),
        ]

    def wait_all(copies):
        for copy in copies:
            copy.wait_recv()

    own_edges = edges(pl.ds(DEEP, cx))

    for side, slot, positions, arrivals in (
        (1, 2 - 2 * odd, (DEEP + cx + 1, DEEP + cx), (direct, (cx - 1, cx - 2))),
        (0, 2 * odd, (DEEP - 1, DEEP - 2), (passed, (0, 1))),
    ):
        for p in arrivals[1]:
            arrivals[0][p].wait_recv()
        for v in range(nvars):
            landed = placed(slot, v, rows_side[side], lanes_side[side])
            for i, q in enumerate(positions):
                part = slice(i * cy, (i + 1) * cy)
                u[q, v, PAD : PAD + cy] = jnp.where(
                    covered_side[side][part] > 0.5, landed[part], u[q, v, PAD : PAD + cy]
                )
    near_edges = edges(pl.ds(DEEP + cx, 2)) + edges(pl.ds(DEEP - 2, 2))

    def section(src, shift, low, height, store, start, stop):
        def plane(q, carry):
            centers = [src[q, v, low : low + height] for v in range(nvars)]
            for v in range(nvars):
                total = coef[v, 3] * centers[v]
                for k in (0, 1, 2, 4, 5, 6):
                    total = total + coef[v, k] * src[q + (k - 3), v, low : low + height]
                    total = total + coef[v, 7 + k] * src[
                        q, v, low + k - 3 : low + k - 3 + height
                    ]
                    total = total + coef[v, 14 + k] * pltpu.roll(
                        centers[v], (3 - k) % cz, 1
                    )
                for w in range(nvars):
                    total = total + coef[v, 21 + w] * centers[w]
                store(q, v, centers[v] + total)
            return carry

        lax.fori_loop(start + shift, stop + shift, plane, 0)

    def inner(start, stop):
        def store(q, v, value):
            first[q - REACH, v, PAD - EDGE : PAD + cy + EDGE] = value

        section(u, DEEP, PAD - EDGE, cy + 2 * EDGE, store, start, stop)

    def outer(start, stop):
        def store(q, v, value):
            first[q - REACH, v, PAD : PAD + cy] = value

        section(u, DEEP, PAD, cy, store, start, stop)

    def final(start, stop):
        def store(q, v, value):
            out[v, natural(q - REACH)] = (
                0.5 * u[q + REACH, v, PAD : PAD + cy] + 0.5 * value
            )

        section(first, REACH, PAD, cy, store, start, stop)

    pass_on(2)
    wait_all(own_edges)
    inner(3, cx - 3)
    pass_on(5)
    upper_edges = edges(pl.ds(DEEP + cx + 2, 1))
    wait_all(near_edges)
    inner(1, 3)
    inner(cx - 3, cx - 1)
    pass_on(3)
    passed[2].wait_recv()
    lower_edges = edges(pl.ds(DEEP - 3, 1))
    pass_on(4)
    wait_all(upper_edges)
    inner(cx - 1, cx)
    outer(cx, cx + 3)
    final(cx - 4, cx)
    wait_all(lower_edges)
    inner(0, 1)
    final(3, cx - 4)
    passed[5].wait_recv()
    passed[3].wait_recv()
    outer(-1, 0)
    final(2, 3)
    passed[4].wait_recv()
    outer(-3, -1)
    final(0, 2)
    for copy in started:
        copy.wait_send()


def body(
    n_grp, n_brk, field, donors, donor_block, donor_corner, donor_weight, fringe_count,
    fringe_cell, velocity, mixing,
):
    nvars, cx, cy, cz = field.shape
    owners, slots = donor_block.shape[2:]
    hbm = pl.BlockSpec(memory_space=pltpu.HBM)
    f32 = jnp.float32
    i32 = jnp.int32
    nsem = 2 * n_brk + 28
    rows = cy + 2 * PAD
    return pl.pallas_call(
        functools.partial(kernel, n_grp, n_brk),
        out_shape=jax.ShapeDtypeStruct(field.shape, f32),
        in_specs=[hbm] * 9,
        out_specs=pl.BlockSpec(memory_space=pltpu.VMEM),
        scratch_shapes=[
            pltpu.VMEM((cx, nvars, cy, cz), f32),
            pltpu.VMEM(donors.shape, f32),
            pltpu.VMEM((owners, slots), i32),
            pltpu.VMEM((owners, slots), i32),
            pltpu.VMEM((3, owners, slots), f32),
            pltpu.SMEM((owners,), i32),
            pltpu.VMEM((owners, slots), i32),
            pltpu.SMEM(velocity.shape, f32),
            pltpu.SMEM(mixing.shape, f32),
            pltpu.VMEM((owners, 8, slots), f32),
            pltpu.VMEM((owners, 8, slots), f32),
            pltpu.VMEM((owners + 2, 8, slots), f32),
            pltpu.VMEM((owners, 3, 8, slots), f32),
            pltpu.VMEM((owners, slots), i32),
            pltpu.VMEM((2, owners, slots), i32),
            pltpu.VMEM((donors.shape[1], 4 * donors.shape[0]), jnp.bfloat16),
            pltpu.VMEM((cx * cy, owners * slots), jnp.bfloat16),
            pltpu.VMEM((cz, owners * slots), jnp.bfloat16),
            pltpu.VMEM((2, 2 * cy, owners * slots), jnp.bfloat16),
            pltpu.VMEM((2, cz, owners * slots), jnp.bfloat16),
            pltpu.VMEM((cx + 2 * DEEP, nvars, rows, cz), f32),
            pltpu.VMEM((cx + 2 * REACH, nvars, rows, cz), f32),
            pltpu.VMEM((2, nvars, cy, cz), f32),
            pltpu.SMEM((nvars, 21 + nvars), f32),
            pltpu.SemaphoreType.DMA((8 + cx,)),
            pltpu.SemaphoreType.DMA((nsem,)),
            pltpu.SemaphoreType.DMA((nsem,)),
        ],
        compiler_params=pltpu.CompilerParams(
            collective_id=0, has_side_effects=True, vmem_limit_bytes=32 << 20
        ),
    )(
        *[
            pltpu.with_memory_space_constraint(x, pltpu.HBM)
            for x in (
                field, donors, donor_block.reshape(owners, slots),
                donor_corner.reshape(owners, slots), donor_weight.reshape(3, owners, slots),
                fringe_count.reshape(owners), fringe_cell.reshape(owners, slots), velocity,
                mixing,
            )
        ]
    )


def solution(mesh):
    placed = (
        P(None, "brk", "grp", None),
        P(("grp", "brk"), None),
        P("grp", "brk", None, None),
        P("grp", "brk", None, None),
        P(None, "grp", "brk", None, None),
        P("grp", "brk", None),
        P("grp", "brk", None, None),
        P(),
        P(),
    )
    return jax.shard_map(
        functools.partial(body, mesh.shape["grp"], mesh.shape["brk"]),
        mesh=mesh, in_specs=placed, out_specs=P(None, "brk", "grp", None), check_vma=False,
    )
```

time: 37.2 us -> 33.9 us (0.911)
  Pallas kernels: 36.2 us -> 32.6 us
    pallas_call x1, Pallas kernels: 36.2 us -> 32.6 us  [body(): pl.pallas_call(functools.partial(kernel, n_grp, n_brk), out_shape=jax.Sha...]
where the time goes in v2:
time: 33.9 us; the launch traced here: 33.5 us
  Pallas kernels  32.6 us (96%)
  local copies, waits for them, and re-layouts  0.84 us (2%)
    pallas_call x1, Pallas kernels, body(): pl.pallas_call(functools.partial(kernel, n_grp, n_brk), out_shape=jax.Sha...  32.6 us
    unnamed x1, local copies, waits for them, and re-layouts  0.84 us

profile of v2, /device:TPU:0, one launch (start us, length us, event | category | flops | bytes accessed | tf_op | source)
XLA Modules:
  0.0 33.5 jit_solution(14423480957910340542)
XLA Ops:
  0.0 32.6 %shard_map.91 = f32[5,8,32,128]{3,2,1,0:T(8,128)S(1)} custom-call(f32[5,8,32,128]{3,2,1,0:T(8,128)} %field_in.1, f32[32,640]{1,0:T(8,128)} %donors_in.1, s32[8,128]{1,0:T(8,128)} %bitcast.6, s32[8,128]{1,0:T(8,128)} %bitcast.7, f32[3,8,128]{2,1,0:T(8,128)} %bitcast.5, s32[8]{0:T(128)} %bitcast.9, s32[8,128]{1,0:T(8,128)} %bitcast.8, f32[3,5]{1,0:T(4,128)} %velocity_in.1, ...), custom_call_target="tpu_custom_call" | custom-call | tf_op jit(solution)/shard_map/pallas_call | solution.py:362
  32.7 0.8 %copy.11 = f32[5,8,32,128]{3,2,1,0:T(8,128)} copy(f32[5,8,32,128]{3,2,1,0:T(8,128)S(1)} %shard_map.91) | data formatting | bytes 1310720

commit v3 on v2

v3 whole, which is shorter than its diff:
```python
import functools

import jax
import jax.numpy as jnp
from jax import lax
from jax.experimental import pallas as pl
from jax.experimental.pallas import tpu as pltpu
from jax.sharding import PartitionSpec as P

time_step = 0.3
PLUS = (-2.0 / 60, 15.0 / 60, -60.0 / 60, 20.0 / 60, 30.0 / 60, -3.0 / 60, 0.0)
MINUS = (0.0, 3.0 / 60, -30.0 / 60, -20.0 / 60, 60.0 / 60, -15.0 / 60, 2.0 / 60)
NT = (((1,), (1,)), ((), ()))
REACH = 3
DEEP = 2 * REACH
EDGE = 8
PAD = 2 * EDGE


def factors(low, weight, count):
    return [
        jnp.where(low == c, 1.0 - weight, jnp.where(low == c - 1, weight, 0.0))
        for c in range(count)
    ]


def kernel(
    n_grp, n_brk, field_in, donors_in, blk_in, corner_in, weight_in, counts_in, cells_in,
    velocity_in, mixing_in, out, field, donors, blk, corner, weight, counts, cells, velocity,
    mixing, req, req_in, res, val_in, cell_out, cell_in, turned, rows_hot, lanes_hot, rows_far,
    rows_near, lanes_side, landed_far, landed_near, u, first, blend, near, far, own_out, own_in,
    upper_out, upper_in, lower_out, lower_in, coef, in_sems, send_sems, recv_sems,
):
    nvars, cx, cy, cz = field_in.shape
    nblk = donors.shape[0]
    block = donors.shape[1] // nvars
    slots = cz
    g = lax.axis_index("grp")
    b = lax.axis_index("brk")
    odd = lax.rem(b, 2)
    partner = b + 1 - 2 * odd
    other = lax.rem(b + n_brk - 1 + 2 * odd, n_brk)
    onward = lax.rem(b + n_brk + 2 - 4 * odd, n_brk)
    up_g, down_g = lax.rem(g + 1, n_grp), lax.rem(g + n_grp - 1, n_grp)

    def natural(p):
        return p + odd * (cx - 1 - 2 * p)

    loads = [
        pltpu.make_async_copy(src, dst, in_sems.at[i])
        for i, (src, dst) in enumerate(
            [(blk_in, blk), (corner_in, corner), (weight_in, weight)]
            + [(field_in.at[:, natural(p)], field.at[p]) for p in (0, 1)]
            + [
                (donors_in, donors), (counts_in, counts), (cells_in, cells),
                (velocity_in, velocity), (mixing_in, mixing),
            ]
            + [(field_in.at[:, natural(p)], field.at[p]) for p in range(2, cx)]
        )
    ]
    for load in loads:
        load.start()

    barrier = pltpu.get_barrier_semaphore()
    for k in range(1, n_brk):
        pl.semaphore_signal(
            barrier, inc=1, device_id=(g, lax.rem(b + k, n_brk)),
            device_id_type=pl.DeviceIdType.MESH,
        )
    for where in (up_g, down_g):
        pl.semaphore_signal(
            barrier, inc=1, device_id=(where, b), device_id_type=pl.DeviceIdType.MESH
        )

    own_pack, upper_pack, lower_pack = (
        (own_out, own_in), (upper_out, upper_in), (lower_out, lower_in)
    )
    index = [0]
    started = []

    def send(src, dst, where):
        i = index[0]
        index[0] = i + 1
        copy = pltpu.make_async_remote_copy(
            src_ref=src, dst_ref=dst, send_sem=send_sems.at[i], recv_sem=recv_sems.at[i],
            device_id=where, device_id_type=pl.DeviceIdType.MESH,
        )
        copy.start()
        started.append(copy)
        return copy

    for load in loads[:3]:
        load.wait()
    for o in range(n_brk):
        req[o, 0] = blk[o : o + 1].astype(jnp.float32)
        req[o, 1] = corner[o : o + 1].astype(jnp.float32)
        for d in range(3):
            req[o, 2 + d] = weight[d, o : o + 1]
    for load in loads[3:5]:
        load.wait()
    pl.semaphore_wait(barrier, n_brk + 1)

    asks = []
    for k in range(1, n_brk):
        o = lax.rem(b + k, n_brk)
        asks.append(send(req.at[o], req_in.at[b], (g, o)))
    mirror = DEEP + 2 * cx - 1
    direct = {}

    def give(src, p, low=0, high=nvars):
        part = pl.ds(low, high - low)
        direct.setdefault(p, []).append(
            send(src.at[p, part], near.at[p, part], (g, partner))
        )

    passed = {}

    def wait_all(copies):
        for copy in copies:
            copy.wait_recv()

    def pass_on(p):
        wait_all(direct[p])
        passed[p] = send(near.at[p], far.at[p], (g, onward))

    def keep(p, low, high):
        for v in range(nvars):
            u[mirror - p, v, PAD + low : PAD + high] = near[p, v, low:high]

    def take(p):
        passed[p].wait_recv()
        for v in range(nvars):
            u[DEEP - 1 - p, v, PAD : PAD + cy] = far[p, v]

    give(field, 0)
    give(field, 1)
    for load in loads[5:]:
        load.wait()
    req_in[b] = req[b]
    slot_id = lax.broadcasted_iota(jnp.int32, (1, slots), 1)
    for o in range(n_brk):
        cell_out[o : o + 1] = jnp.where(slot_id < counts[o], cells[o : o + 1], -1)
    for v in range(nvars):
        center = 0.0
        for d in range(3):
            speed = velocity[d, v]
            fast = jnp.maximum(speed, 0.0) * (-time_step)
            slow = jnp.minimum(speed, 0.0) * (-time_step)
            for k in range(7):
                value = fast * PLUS[k] + slow * MINUS[k]
                if d == 0:
                    value = jnp.where(odd == 1, fast * PLUS[6 - k] + slow * MINUS[6 - k], value)
                if k == 3:
                    center = center + value
                else:
                    coef[v, d * 7 + k] = value
        coef[v, 3] = 1.0 + center + mixing[v, v] * (-time_step)
        for w in range(nvars):
            coef[v, 21 + w] = mixing[v, w] * (-time_step)
    cells_sent = [
        send(cell_out, cell_in.at[0], (g, other)), send(cell_out, cell_in.at[1], (g, partner))
    ]

    whole = donors[...]
    one = whole.astype(jnp.bfloat16).astype(jnp.float32)
    two = (whole - one).astype(jnp.bfloat16).astype(jnp.float32)
    three = whole - one - two
    stacked = jnp.concatenate([one, two, three, jnp.zeros_like(whole)], axis=0)
    turned[...] = jnp.transpose(stacked).astype(jnp.bfloat16)

    def mark(targets_ref, flip, planes, rows_ref, lanes_ref):
        row_id = lax.broadcasted_iota(jnp.int32, (len(planes) * cy, slots), 0)
        label = row_id + planes[0] * cy
        for i in range(1, len(planes)):
            jump = planes[i] - planes[i - 1] - 1
            if jump:
                label = label + jnp.where(row_id >= i * cy, jump * cy, 0)
        lane_id = lax.broadcasted_iota(jnp.int32, (cz, slots), 0)
        for o in range(n_brk):
            cell = targets_ref[o : o + 1]
            row = cell // cz
            x = row // cy
            row = jnp.where(cell < 0, -1, row + flip * (cx - 1 - 2 * x) * cy)
            part = slice(o * slots, (o + 1) * slots)
            rows_ref[:, part] = jnp.where(label == row, 1.0, 0.0).astype(jnp.bfloat16)
            lanes_ref[:, part] = jnp.where(lane_id == cell % cz, 1.0, 0.0).astype(jnp.bfloat16)
        return lax.dot_general(
            rows_ref[...], lanes_ref[...], NT, preferred_element_type=jnp.float32
        )

    covered = mark(cell_out, odd, range(cx), rows_hot, lanes_hot)

    block_id = lax.broadcasted_iota(jnp.int32, (4 * nblk, slots), 0) % nblk

    def interpolated(r):
        asked = req_in[r]
        wanted = asked[0].astype(jnp.int32)
        low = asked[1].astype(jnp.int32)
        hot = jnp.where(block_id == wanted, 1.0, 0.0).astype(jnp.bfloat16)
        picked = jnp.dot(turned[...], hot, preferred_element_type=jnp.float32)
        fx = factors(low // 32, asked[2], 4)
        fy = factors((low // 8) % 4, asked[3], 4)
        z_id = lax.broadcasted_iota(jnp.int32, (8, slots), 0)
        low_z = low % 8
        wz = asked[4]
        fz = jnp.where(z_id == low_z, 1.0 - wz, jnp.where(z_id == low_z + 1, wz, 0.0))
        tables = [fx[i] * fy[j] * fz for i in range(4) for j in range(4)]
        sums = []
        for v in range(nvars):
            total = None
            for i, table in enumerate(tables):
                start = v * block + 8 * i
                term = picked[start : start + 8] * table
                total = term if total is None else total + term
            sums.append(jnp.sum(total, axis=0, keepdims=True))
        for v in range(nvars):
            res[r + 1, v] = sums[v]

    for k in range(n_brk):
        if k > 0:
            asks[k - 1].wait_recv()
        if k == n_brk // 2:
            give(field, 2, 0, 3)
        r = lax.rem(b + n_brk - k, n_brk)
        interpolated(r)
    res[0] = res[n_brk]
    res[n_brk + 1] = res[1]
    answers = []
    for k in range(1, n_brk):
        o = lax.rem(b + k, n_brk)
        answers.append(send(res.at[pl.ds(o, 3)], val_in.at[b], (g, o)))
    for slot in range(3):
        val_in[b, slot] = res[b + slot]

    raw_planes = ((0, 1, 2, 3, 5), (2, 3, 5))
    rows_of = (rows_far, rows_near)
    covered_side = []
    for side in range(2):
        cells_sent[side].wait_recv()
        covered_side.append(
            mark(
                cell_in.at[side], 1 - odd, raw_planes[side], rows_of[side], lanes_side.at[side]
            )
        )
    pass_on(0)
    give(field, 2, 3)
    give(field, 5)
    give(field, 3)
    pass_on(1)
    for pending in answers:
        pending.wait_recv()

    def placed(slot, v, rows, lanes):
        row = jnp.concatenate([val_in[o, slot, v] for o in range(n_brk)], axis=1)
        high = row.astype(jnp.bfloat16)
        rest = (row - high.astype(jnp.float32)).astype(jnp.bfloat16)
        spread = jnp.concatenate([lanes * high, lanes * rest], axis=0)
        both = lax.dot_general(rows, spread, NT, preferred_element_type=jnp.float32)
        return both[:, :cz] + both[:, cz:]

    for v in range(nvars):
        landed = placed(1, v, rows_hot[...], lanes_hot[...])
        for p in range(cx):
            part = slice(p * cy, (p + 1) * cy)
            plane = jnp.where(covered[part] > 0.5, landed[part], field[p, v])
            u[DEEP + p, v, PAD : PAD + cy] = plane
            if p in (4, cx - 2, cx - 1):
                blend[p, v] = plane
    faces = pl.ds(cx - 2, 2)

    def give_rows(low, height):
        part = (faces, slice(None), pl.ds(low, height))
        return send(blend.at[part], near.at[part], (g, partner))

    give(blend, 4)
    outer_rows = [give_rows(0, EDGE), give_rows(cy - EDGE, EDGE)]
    inner_rows = [give_rows(EDGE, cy - 2 * EDGE)]

    def edges(packs, q0):
        out_pack, in_pack = packs
        _, count, _, steps, step, _ = out_pack.shape
        for i in range(count):
            for v in range(nvars):
                for k in range(steps):
                    top = PAD + cy + (k - steps) * step
                    low = PAD + k * step
                    out_pack[0, i, v, k] = u[q0 + i, v, top : top + step]
                    out_pack[1, i, v, k] = u[q0 + i, v, low : low + step]
        return [
            send(out_pack.at[0], in_pack.at[0], (up_g, b)),
            send(out_pack.at[1], in_pack.at[1], (down_g, b)),
        ]

    def land(copies, packs, q0):
        wait_all(copies)
        in_pack = packs[1]
        _, count, _, steps, step, _ = in_pack.shape
        for i in range(count):
            for v in range(nvars):
                for k in range(steps):
                    low = PAD + (k - steps) * step
                    top = PAD + cy + k * step
                    u[q0 + i, v, low : low + step] = in_pack[0, i, v, k]
                    u[q0 + i, v, top : top + step] = in_pack[1, i, v, k]

    own_edges = edges(own_pack, DEEP)

    pass_on(2)
    landed_of = (landed_far, landed_near)
    for side, slot in ((1, 2 - 2 * odd), (0, 2 * odd)):
        for v in range(nvars):
            landed_of[side][v] = placed(slot, v, rows_of[side][...], lanes_side[side])

    def settle(side, raw, wanted):
        for p in wanted:
            i = raw_planes[side].index(p)
            q = mirror - p if side else DEEP - 1 - p
            part = slice(i * cy, (i + 1) * cy)
            for v in range(nvars):
                u[q, v, PAD : PAD + cy] = jnp.where(
                    covered_side[side][part] > 0.5, landed_of[side][v, part], raw[p, v]
                )

    def section(src, shift, low, height, store, start, stop):
        def group(first_q, count):
            for v in range(nvars):
                c = [coef[v, k] for k in range(21 + nvars)]
                for q in [first_q + n for n in range(count)]:
                    mid = src[q, v, low : low + height]
                    total = c[3] * mid
                    for k in (0, 1, 2, 4, 5, 6):
                        total = total + c[k] * src[q + (k - 3), v, low : low + height]
                        total = total + c[7 + k] * src[
                            q, v, low + k - 3 : low + k - 3 + height
                        ]
                        total = total + c[14 + k] * pltpu.roll(mid, (3 - k) % cz, 1)
                    for w in range(nvars):
                        if w != v:
                            total = total + c[21 + w] * src[q, w, low : low + height]
                    store(q, v, total)

        q = start + shift
        while q < stop + shift:
            count = min(3, stop + shift - q)
            group(q, count)
            q = q + count

    def inner(start, stop):
        def store(q, v, value):
            first[q - REACH, v, PAD - EDGE : PAD + cy + EDGE] = value

        section(u, DEEP, PAD - EDGE, cy + 2 * EDGE, store, start, stop)

    def outer(start, stop):
        def store(q, v, value):
            first[q - REACH, v, PAD : PAD + cy] = value

        section(u, DEEP, PAD, cy, store, start, stop)

    def final(start, stop):
        def store(q, v, value):
            out[v, natural(q - REACH)] = (
                0.5 * u[q + REACH, v, PAD : PAD + cy] + 0.5 * value
            )

        section(first, REACH, PAD, cy, store, start, stop)

    pass_on(5)
    pass_on(3)
    settle(1, near, (2, 3, 5))
    wait_all([passed[0], passed[1]])
    settle(0, far, (0, 1))
    wait_all([passed[2]])
    settle(0, far, (2,))
    lower_edges = edges(lower_pack, DEEP - REACH)
    land(own_edges, own_pack, DEEP)
    inner(3, cx - 3)
    wait_all(outer_rows)
    for p in (cx - 2, cx - 1):
        keep(p, 0, EDGE)
        keep(p, cy - EDGE, cy)
    upper_edges = edges(upper_pack, DEEP + cx)
    pass_on(4)
    keep(4, 0, cy)
    land(lower_edges, lower_pack, DEEP - REACH)
    inner(0, 3)
    wait_all([passed[5], passed[3]])
    settle(0, far, (5, 3))
    outer(-1, 0)
    land(upper_edges, upper_pack, DEEP + cx)
    wait_all(inner_rows)
    for p in (cx - 2, cx - 1):
        keep(p, EDGE, cy - EDGE)
    inner(cx - 3, cx)
    outer(cx, cx + 3)
    final(2, cx)
    early = len(started) - 2
    for copy in started[:early]:
        copy.wait_send()
    take(4)
    outer(-3, -1)
    final(0, 2)
    for copy in started[early:]:
        copy.wait_send()


def body(
    n_grp, n_brk, field, donors, donor_block, donor_corner, donor_weight, fringe_count,
    fringe_cell, velocity, mixing,
):
    nvars, cx, cy, cz = field.shape
    owners, slots = donor_block.shape[2:]
    hbm = pl.BlockSpec(memory_space=pltpu.HBM)
    f32 = jnp.float32
    i32 = jnp.int32
    nsem = 2 * n_brk + 29
    rows = cy + 2 * PAD
    field_brick = (cx, nvars, cy, cz)
    return pl.pallas_call(
        functools.partial(kernel, n_grp, n_brk),
        out_shape=jax.ShapeDtypeStruct(field.shape, f32),
        in_specs=[hbm] * 9,
        out_specs=pl.BlockSpec(memory_space=pltpu.VMEM),
        scratch_shapes=[
            pltpu.VMEM(field_brick, f32),
            pltpu.VMEM(donors.shape, f32),
            pltpu.VMEM((owners, slots), i32),
            pltpu.VMEM((owners, slots), i32),
            pltpu.VMEM((3, owners, slots), f32),
            pltpu.SMEM((owners,), i32),
            pltpu.VMEM((owners, slots), i32),
            pltpu.SMEM(velocity.shape, f32),
            pltpu.SMEM(mixing.shape, f32),
            pltpu.VMEM((owners, 5, 1, slots), f32),
            pltpu.VMEM((owners, 5, 1, slots), f32),
            pltpu.VMEM((owners + 2, nvars, 1, slots), f32),
            pltpu.VMEM((owners, 3, nvars, 1, slots), f32),
            pltpu.VMEM((owners, slots), i32),
            pltpu.VMEM((2, owners, slots), i32),
            pltpu.VMEM((donors.shape[1], 4 * donors.shape[0]), jnp.bfloat16),
            pltpu.VMEM((cx * cy, owners * slots), jnp.bfloat16),
            pltpu.VMEM((cz, owners * slots), jnp.bfloat16),
            pltpu.VMEM((5 * cy, owners * slots), jnp.bfloat16),
            pltpu.VMEM((3 * cy, owners * slots), jnp.bfloat16),
            pltpu.VMEM((2, cz, owners * slots), jnp.bfloat16),
            pltpu.VMEM((nvars, 5 * cy, cz), f32),
            pltpu.VMEM((nvars, 3 * cy, cz), f32),
            pltpu.VMEM((cx + 2 * DEEP, nvars, rows, cz), f32),
            pltpu.VMEM((cx + 2 * REACH, nvars, rows, cz), f32),
            pltpu.VMEM(field_brick, f32),
            pltpu.VMEM(field_brick, f32),
            pltpu.VMEM((DEEP, nvars, cy, cz), f32),
            pltpu.VMEM((2, cx, nvars, DEEP // 2, 2, cz), f32),
            pltpu.VMEM((2, cx, nvars, DEEP // 2, 2, cz), f32),
            pltpu.VMEM((2, REACH, nvars, REACH, 1, cz), f32),
            pltpu.VMEM((2, REACH, nvars, REACH, 1, cz), f32),
            pltpu.VMEM((2, REACH, nvars, REACH, 1, cz), f32),
            pltpu.VMEM((2, REACH, nvars, REACH, 1, cz), f32),
            pltpu.SMEM((nvars, 21 + nvars), f32),
            pltpu.SemaphoreType.DMA((8 + cx,)),
            pltpu.SemaphoreType.DMA((nsem,)),
            pltpu.SemaphoreType.DMA((nsem,)),
        ],
        compiler_params=pltpu.CompilerParams(
            collective_id=0, has_side_effects=True, vmem_limit_bytes=32 << 20
        ),
    )(
        *[
            pltpu.with_memory_space_constraint(x, pltpu.HBM)
            for x in (
                field, donors, donor_block.reshape(owners, slots),
                donor_corner.reshape(owners, slots), donor_weight.reshape(3, owners, slots),
                fringe_count.reshape(owners), fringe_cell.reshape(owners, slots), velocity,
                mixing,
            )
        ]
    )


def solution(mesh):
    placed = (
        P(None, "brk", "grp", None),
        P(("grp", "brk"), None),
        P("grp", "brk", None, None),
        P("grp", "brk", None, None),
        P(None, "grp", "brk", None, None),
        P("grp", "brk", None),
        P("grp", "brk", None, None),
        P(),
        P(),
    )
    return jax.shard_map(
        functools.partial(body, mesh.shape["grp"], mesh.shape["brk"]),
        mesh=mesh, in_specs=placed, out_specs=P(None, "brk", "grp", None), check_vma=False,
    )
```

time: 33.9 us -> 29.1 us (0.86)
  the two profiles are of different devices: /device:TPU:0 before, /device:TPU:3 now
where the time goes in v3:
time: 29.1 us; the launch traced here: 28.9 us
  Pallas kernels  28.1 us (97%)
  local copies, waits for them, and re-layouts  0.84 us (3%)
    pallas_call x1, Pallas kernels, body(): pl.pallas_call(functools.partial(kernel, n_grp, n_brk), out_shape=jax.Sha...  28.1 us
    unnamed x1, local copies, waits for them, and re-layouts  0.84 us

profile of v3, /device:TPU:3, one launch (start us, length us, event | category | flops | bytes accessed | tf_op | source)
XLA Modules:
  0.0 28.9 jit_solution(14905529103359194250)
XLA Ops:
  0.0 28.1 %shard_map.91 = f32[5,8,32,128]{3,2,1,0:T(8,128)S(1)} custom-call(f32[5,8,32,128]{3,2,1,0:T(8,128)} %field_in.1, f32[32,640]{1,0:T(8,128)} %donors_in.1, s32[8,128]{1,0:T(8,128)} %bitcast.6, s32[8,128]{1,0:T(8,128)} %bitcast.7, f32[3,8,128]{2,1,0:T(8,128)} %bitcast.5, s32[8]{0:T(128)} %bitcast.9, s32[8,128]{1,0:T(8,128)} %bitcast.8, f32[3,5]{1,0:T(4,128)} %velocity_in.1, ...), custom_call_target="tpu_custom_call" | custom-call | tf_op jit(solution)/shard_map/pallas_call | solution.py:419
  28.1 0.8 %copy.11 = f32[5,8,32,128]{3,2,1,0:T(8,128)} copy(f32[5,8,32,128]{3,2,1,0:T(8,128)S(1)} %shard_map.91) | data formatting | bytes 1310720

commit v4 on v3

--- a/solution.py
+++ b/solution.py
@@ -220,7 +220,7 @@
         if k > 0:
             asks[k - 1].wait_recv()
         if k == n_brk // 2:
-            give(field, 2, 0, 3)
+            give(field, 2)
         r = lax.rem(b + n_brk - k, n_brk)
         interpolated(r)
     res[0] = res[n_brk]
@@ -243,7 +243,6 @@
             )
         )
     pass_on(0)
-    give(field, 2, 3)
     give(field, 5)
     give(field, 3)
     pass_on(1)

time: 29.1 us -> 29.1 us (level)
  no operation moved by 1% of the time
where the time goes in v4:
time: 29.1 us; the launch traced here: 28.9 us
  Pallas kernels  28.1 us (97%)
  local copies, waits for them, and re-layouts  0.84 us (3%)
    pallas_call x1, Pallas kernels, body(): pl.pallas_call(functools.partial(kernel, n_grp, n_brk), out_shape=jax.Sha...  28.1 us
    unnamed x1, local copies, waits for them, and re-layouts  0.84 us

profile of v4, /device:TPU:3, one launch (start us, length us, event | category | flops | bytes accessed | tf_op | source)
XLA Modules:
  0.0 28.9 jit_solution(13748611265530110999)
XLA Ops:
  0.0 28.1 %shard_map.91 = f32[5,8,32,128]{3,2,1,0:T(8,128)S(1)} custom-call(f32[5,8,32,128]{3,2,1,0:T(8,128)} %field_in.1, f32[32,640]{1,0:T(8,128)} %donors_in.1, s32[8,128]{1,0:T(8,128)} %bitcast.6, s32[8,128]{1,0:T(8,128)} %bitcast.7, f32[3,8,128]{2,1,0:T(8,128)} %bitcast.5, s32[8]{0:T(128)} %bitcast.9, s32[8,128]{1,0:T(8,128)} %bitcast.8, f32[3,5]{1,0:T(4,128)} %velocity_in.1, ...), custom_call_target="tpu_custom_call" | custom-call | tf_op jit(solution)/shard_map/pallas_call | solution.py:418
  28.1 0.8 %copy.11 = f32[5,8,32,128]{3,2,1,0:T(8,128)} copy(f32[5,8,32,128]{3,2,1,0:T(8,128)S(1)} %shard_map.91) | data formatting | bytes 1310720
